TPU v7x, 512 devices: a whole 4x8x8 slice. The times are simulated.
512 devices in a mesh: dp: 128 (over z_lo, x, y), mp: 4 (over z_hi, core).
Axes of the slice: x: 4, y: 8, z: 8 (z_hi: 2, z_lo: 4; z = z_hi * 4 + z_lo), core: 2. Of those that a mesh axis runs over, the one named last changes fastest.
Arguments:
- images: bfloat16 [24576, 1024], P('dp', 'mp'), may hold values from -80 to 80, as said below
- texts: bfloat16 [24576, 1024], P('dp', 'mp'), may hold values from -80 to 80, as said below
- logit_scale: float32 [1], replicated, may hold values from 240 to 300
Outputs:
- row_loss: float32 [24576], P('dp')
- column_loss: float32 [24576], P('dp')
Inputs may be any that keep to these rules, and one draw needn't show every extreme that they name: `images`: Real-valued entries. `texts`: Real-valued entries.
All inputs are finite; a program needn't handle non-finite values.
Results may differ from a plain program's by a relative error of at most 0.0044.
Values may be sent and summed in bfloat16 or wider, within the bound.
A program may use at most 64 MiB of HBM per device.

v0:
```python
import jax
import jax.numpy as jnp
from jax import lax
from jax.sharding import Mesh
from jax.sharding import PartitionSpec as P

DP = ("dp_0", "dp_1", "dp_2")


def joined_along(parts, dim):
    parts = jnp.moveaxis(parts, 0, dim)
    lengths = parts.shape
    return parts.reshape(*lengths[:dim], lengths[dim] * lengths[dim + 1], *lengths[dim + 2 :])


def sent_to_all(x, axis):
    copies = jnp.broadcast_to(x, (lax.axis_size(axis), *x.shape))
    return lax.all_to_all(copies, axis, split_axis=0, concat_axis=0, tiled=True)


def gathered_copies(x, axis, dim):
    return joined_along(sent_to_all(x, axis), dim)


def all_blocks(x, axes, order):
    parts = x
    for k in order:
        parts = lax.all_gather(parts, axes[k])
    done = order[::-1]
    back = [done.index(k) for k in range(len(axes))]
    parts = parts.transpose(*back, *range(len(axes), parts.ndim))
    return parts.reshape(-1, *x.shape)


def gather_axes(x, axes, order, dim):
    return joined_along(all_blocks(x, axes, order), dim)


def side_by_side(arrays, axis, split_dim, concat_dim, along):
    ends, at = ([], 0)
    for a in arrays[:-1]:
        at += a.shape[along]
        ends.append(at)
    both = jnp.concatenate(arrays, axis=along)
    return tuple(
        jnp.split(
            lax.all_to_all(both, axis, split_axis=split_dim, concat_axis=concat_dim, tiled=True),
            ends,
            axis=along,
        )
    )


def taken_together(x, axis):
    return sent_to_all(x, axis).max(axis=0)


def of_everyone(x, axis):
    everything = sent_to_all(x, axis)
    return jnp.sum(everything, axis=0)


def turned_gather(arrays, axis, dims):
    turned = [jnp.moveaxis(a, dim, 0) for a, dim in zip(arrays, dims)]
    widths = [t[0].size for t in turned]
    both = jnp.concatenate([t.reshape(-1, w) for t, w in zip(turned, widths)], axis=1)
    out = lax.all_gather(both, axis, axis=0, tiled=True)
    parts = jnp.split(out, [sum(widths[:k]) for k in range(1, len(widths))], axis=1)
    return tuple(
        (
            jnp.moveaxis(b.reshape(-1, *t.shape[1:]), 0, dim)
            for b, t, dim in zip(parts, turned, dims)
        )
    )


def normalize(rows):
    values = rows.astype(jnp.float32)
    return (values * lax.rsqrt(jnp.sum(values * values, axis=1, keepdims=True) + 1e-06)).astype(
        jnp.bfloat16
    )


def tile_states(visitor, image_unit, inverse_temp):
    scores = inverse_temp * lax.dot_general(
        visitor, image_unit, (((1,), (1,)), ((), ())), preferred_element_type=jnp.float32
    )
    column_top = jnp.max(scores, axis=1)
    column_total = jnp.sum(jnp.exp(scores - column_top[:, None]), axis=1)
    row_top = jnp.max(scores, axis=0)
    row_total = jnp.sum(jnp.exp(scores - row_top[None, :]), axis=0)
    return (column_top, column_total, row_top, row_total)


def merge_rows(row_top, other_top, other_total):
    new_top = jnp.maximum(row_top, other_top)
    return (new_top, other_total * jnp.exp(other_top - new_top))


def on_device(images, texts, logit_scale):
    cycle_count = lax.axis_size(DP)
    mp_pos = lax.axis_index("mp")
    full_images = gathered_copies(images, "mp", 1)
    own_texts = lax.all_to_all(texts, "mp", split_axis=0, concat_axis=1, tiled=True)
    image_unit = normalize(full_images)
    text_unit = normalize(own_texts)
    inverse_temp = logit_scale[0]
    quarter = text_unit.shape[0]
    image_rows = image_unit.shape[0]
    mine = lax.dynamic_slice_in_dim(image_unit, mp_pos * quarter, quarter, 0)
    matched = inverse_temp * jnp.sum(
        mine.astype(jnp.float32) * text_unit.astype(jnp.float32), axis=1
    )
    acc_top = jnp.full((image_rows,), -1e30, jnp.float32)
    col_top, col_total, other_top, other_total = tile_states(
        gather_axes(text_unit, DP, (0, 2, 1), 0), image_unit, inverse_temp
    )
    acc_top, acc_total = merge_rows(acc_top, other_top, other_total)
    store_top = col_top.reshape(cycle_count, quarter)
    store_total = col_total.reshape(cycle_count, quarter)
    got_top, got_total = side_by_side((store_top, store_total), DP, 0, 0, 1)
    column_peak = jnp.max(got_top, axis=0)
    column_lse = column_peak + jnp.log(
        jnp.sum(got_total * jnp.exp(got_top - column_peak[None, :]), axis=0)
    )
    row_peak = taken_together(acc_top, "mp")
    row_whole = of_everyone(acc_total * jnp.exp(acc_top - row_peak), "mp")
    row_lse = row_peak + jnp.log(row_whole)
    column_full, matched_full = turned_gather((column_lse, matched), "mp", (0, 0))
    return (row_lse - matched_full, column_full - matched_full)


def solution(mesh):
    finer = Mesh(mesh.devices.reshape(4, 4, 8, mesh.shape["mp"]), ("dp_0", "dp_1", "dp_2", "mp"))
    return jax.shard_map(
        on_device,
        mesh=finer,
        in_specs=(P(DP, "mp"), P(DP, "mp"), P()),
        out_specs=(P(DP), P(DP)),
        check_vma=False,
    )
```

profile of v0, /device:TPU:1, one launch (start us, length us, event | category | flops | bytes accessed | tf_op | source)
XLA Modules:
  0.0 294.7 jit_solution(13869063874590567412)
XLA Ops:
  7.2 19.1 %all_to_all.42 = bf16[4,48,256]{2,1,0:T(8,128)(2,1)S(1)} all-to-all(bf16[4,48,256]{2,1,0:T(8,128)(2,1)} %bitcast.46), channel_id=1, replica_groups=mesh['dp_0'=4,'dp_1'=4,'dp_2'=8,'mp'=4] {'mp'}, dimensions={0} | all-to-all | bytes 196608 | tf_op jit(solution)/shard_map/all_to_all | solution.py:104
  26.3 0.1 fusion.3
  26.5 0.1 copy.22
  26.6 0.1 reshape.123
  26.7 0.1 multiply_convert_fusion.1
  26.8 13.7 %all_gather.19 = bf16[4,48,1024]{2,1,0:T(8,128)(2,1)} all-gather(bf16[1,48,1024]{2,1,0:T(8,128)(2,1)S(1)} %multiply_convert_fusion.1), channel_id=1, replica_groups=mesh['dp_0'=4,'dp_1'=4,'dp_2'=8,'mp'=4] {'dp_0'}, dimensions={0}, use_global_device_ids=true | all-gather | bytes 491520 | tf_op jit(solution)/shard_map/all_gather | solution.py:28
  40.6 47.3 %all-gather.6.cloned.1.call-done = bf16[32,48,1024]{2,1,0:T(8,128)(2,1)} async-done(((bf16[4,48,1024]{2,1,0:T(8,128)(2,1)}), bf16[32,48,1024]{2,1,0:T(8,128)(2,1)}) %all-gather.6.cloned.1.call-update) | async-done | bytes 3145744 | tf_op jit(solution)/shard_map/all_gather | solution.py:28
  87.9 0.8 broadcast_in_dim.8
  88.7 9.0 %all-to-all-start.1 = ((bf16[4,192,256]{2,1,0:T(8,128)(2,1)}), bf16[4,192,256]{2,1,0:T(8,128)(2,1)S(1)}, u32[]{:S(2)}, u32[]{:S(2)}) async-start(bf16[4,192,256]{2,1,0:T(8,128)(2,1)} %broadcast_in_dim.8), calls=%async_computation.1 | async-start | bytes 786432 | tf_op jit(solution)/shard_map/all_to_all | solution.py:18
  98.4 9.7 %all-to-all-done.1 = bf16[4,192,256]{2,1,0:T(8,128)(2,1)S(1)} async-done(((bf16[4,192,256]{2,1,0:T(8,128)(2,1)}), bf16[4,192,256]{2,1,0:T(8,128)(2,1)S(1)}, u32[]{:S(2)}, u32[]{:S(2)}) %all-to-all-start.1) | async-done | bytes 393248 | tf_op jit(solution)/shard_map/all_to_all | solution.py:18
  108.1 0.2 fusion
  108.3 0.1 dynamic-slice
  108.3 0.1 fusion.2
  108.6 0.1 copy.34
  108.7 0.2 multiply_reduce_fusion
  108.9 104.7 %all-gather.8.cloned.1.call-done = bf16[32,4,48,1024]{3,2,1,0:T(8,128)(2,1)} async-done(((bf16[8,4,48,1024]{3,2,1,0:T(8,128)(2,1)}), bf16[32,4,48,1024]{3,2,1,0:T(8,128)(2,1)}) %all-gather.8.cloned.1.call-update) | async-done | bytes 12582928 | tf_op jit(solution)/shard_map/all_gather | solution.py:28
  213.6 6.3 %copy.23 = bf16[32,4,48,1024]{3,2,0,1:T(8,128)(2,1)S(1)} copy(bf16[32,4,48,1024]{3,2,1,0:T(8,128)(2,1)} %all-gather.8.cloned.1.call-done) | data formatting | bytes 25165824 | tf_op jit(solution)/shard_map/all_gather | solution.py:28
  219.9 6.1 %fusion.6 = (f32[192]{0:T(256)S(1)}, f32[6144]{0:T(1024)S(1)}, f32[6144,192]{0,1:T(8,128)}) fusion(bf16[6144,1024]{1,0:T(8,128)(2,1)S(1)} %bitcast.39, bf16[192,1024]{1,0:T(8,128)(2,1)S(1)} %bitcast.45, f32[]{:T(128)} %bitcast.37), kind=kOutput, calls=%fused_computation.30 | convolution fusion | flops 2419451648 | bytes 17720068 | tf_op jit(solution)/shard_map/dot_general | solution.py:85
  226.0 0.6 broadcast_in_dim.19
  226.6 8.2 %all-to-all-start.2 = ((f32[4,1,192]{2,1,0:T(1,128)}), f32[4,1,192]{2,1,0:T(1,128)S(1)}, u32[]{:S(2)}, u32[]{:S(2)}) async-start(f32[4,1,192]{2,1,0:T(1,128)} %broadcast_in_dim.19), calls=%async_computation.2 | async-start | bytes 8192 | tf_op jit(solution)/shard_map/all_to_all | solution.py:18
  234.8 3.7 %exponential_reduce_fusion.1 = (f32[192]{0:T(256)S(1)}, f32[6144]{0:T(1024)S(1)}) fusion(f32[6144,192]{0,1:T(8,128)} %get-tuple-element.12, f32[192]{0:T(256)S(1)} %get-tuple-element.4, f32[6144]{0:T(1024)S(1)} %get-tuple-element.5), kind=kLoop, calls=%fused_computation.2 | loop fusion | flops 4712256 | bytes 4769280 | tf_op jit(solution)/shard_map/reduce_sum | solution.py:91
  238.7 3.1 %all-to-all-done.2 = f32[4,1,192]{2,1,0:T(1,128)S(1)} async-done(((f32[4,1,192]{2,1,0:T(1,128)}), f32[4,1,192]{2,1,0:T(1,128)S(1)}, u32[]{:S(2)}, u32[]{:S(2)}) %all-to-all-start.2) | async-done | bytes 3104 | tf_op jit(solution)/shard_map/all_to_all | solution.py:18
  241.8 0.6 broadcast_in_dim.20
  242.4 4.1 %all-to-all-start.3 = ((f32[4,1,192]{2,1,0:T(1,128)}), f32[4,1,192]{2,1,0:T(1,128)S(1)}, u32[]{:S(2)}, u32[]{:S(2)}) async-start(f32[4,1,192]{2,1,0:T(1,128)} %broadcast_in_dim.20), calls=%async_computation.3 | async-start | bytes 8192 | tf_op jit(solution)/shard_map/all_to_all | solution.py:18
  246.6 0.7 pad_maximum_fusion
  247.3 6.3 %all-to-all-done.3 = f32[4,1,192]{2,1,0:T(1,128)S(1)} async-done(((f32[4,1,192]{2,1,0:T(1,128)}), f32[4,1,192]{2,1,0:T(1,128)S(1)}, u32[]{:S(2)}, u32[]{:S(2)}) %all-to-all-start.3) | async-done | bytes 3104 | tf_op jit(solution)/shard_map/all_to_all | solution.py:18
  253.6 11.4 %all-to-all-start.4 = ((f32[128,1,96]{2,1,0:T(1,128)}), f32[128,1,96]{2,1,0:T(1,128)S(1)}, u32[]{:S(2)}, u32[]{:S(2)}) async-start(f32[128,1,96]{2,1,0:T(1,128)} %bitcast.9), calls=%async_computation.4 | async-start | bytes 131072 | tf_op jit(solution)/shard_map/all_to_all | solution.py:47
  265.0 11.1 %all-to-all-done.4 = f32[128,1,96]{2,1,0:T(1,128)S(1)} async-done(((f32[128,1,96]{2,1,0:T(1,128)}), f32[128,1,96]{2,1,0:T(1,128)S(1)}, u32[]{:S(2)}, u32[]{:S(2)}) %all-to-all-start.4) | async-done | bytes 49184 | tf_op jit(solution)/shard_map/all_to_all | solution.py:47
  276.1 0.1 fusion.5
  276.3 10.9 %all-gather.2 = f32[4,48,2]{1,2,0:T(2,128)S(1)} all-gather(f32[1,48,2]{1,2,0:T(2,128)S(1)} %maximum_bitcast_fusion), channel_id=1, replica_groups=mesh['dp_0'=4,'dp_1'=4,'dp_2'=8,'mp'=4] {'mp'}, dimensions={0}, use_global_device_ids=true | all-gather | bytes 1920 | tf_op jit(solution)/shard_map/all_gather | solution.py:67
  287.2 0.1 reshape.129
  287.3 0.6 fusion.8
  (24 shorter events, 0.6 us)
Async XLA Ops:
  7.2 80.8 %copy-start = (bf16[192,256]{1,0:T(8,128)(2,1)S(1)}, bf16[192,256]{1,0:T(8,128)(2,1)}, u32[]{:S(2)}) copy-start(bf16[192,256]{1,0:T(8,128)(2,1)} %param.3) | copy-start | bytes 294916
  7.2 80.7 %all-gather.6.cloned.1.call-start = ((), (), s32[]{:S(2)}) async-start(), calls=%async_computation.5 | async-start | bytes 3538944 | tf_op jit(solution)/shard_map/all_gather | solution.py:28
  40.5 173.1 %all-gather.8.cloned.1.call-start = ((), (), s32[]{:S(2)}) async-start(), calls=%async_computation.6 | async-start | bytes 15728640 | tf_op jit(solution)/shard_map/all_gather | solution.py:28
  88.7 19.4 %all-to-all-start.1 = ((bf16[4,192,256]{2,1,0:T(8,128)(2,1)}), bf16[4,192,256]{2,1,0:T(8,128)(2,1)S(1)}, u32[]{:S(2)}, u32[]{:S(2)}) async-start(bf16[4,192,256]{2,1,0:T(8,128)(2,1)} %broadcast_in_dim.8), calls=%async_computation.1 | async-start | bytes 786432 | tf_op jit(solution)/shard_map/all_to_all | solution.py:18
  226.6 15.2 %all-to-all-start.2 = ((f32[4,1,192]{2,1,0:T(1,128)}), f32[4,1,192]{2,1,0:T(1,128)S(1)}, u32[]{:S(2)}, u32[]{:S(2)}) async-start(f32[4,1,192]{2,1,0:T(1,128)} %broadcast_in_dim.19), calls=%async_computation.2 | async-start | bytes 8192 | tf_op jit(solution)/shard_map/all_to_all | solution.py:18
  242.4 11.1 %all-to-all-start.3 = ((f32[4,1,192]{2,1,0:T(1,128)}), f32[4,1,192]{2,1,0:T(1,128)S(1)}, u32[]{:S(2)}, u32[]{:S(2)}) async-start(f32[4,1,192]{2,1,0:T(1,128)} %broadcast_in_dim.20), calls=%async_computation.3 | async-start | bytes 8192 | tf_op jit(solution)/shard_map/all_to_all | solution.py:18
  253.6 22.5 %all-to-all-start.4 = ((f32[128,1,96]{2,1,0:T(1,128)}), f32[128,1,96]{2,1,0:T(1,128)S(1)}, u32[]{:S(2)}, u32[]{:S(2)}) async-start(f32[128,1,96]{2,1,0:T(1,128)} %bitcast.9), calls=%async_computation.4 | async-start | bytes 131072 | tf_op jit(solution)/shard_map/all_to_all | solution.py:47
Sparse Core Ops, SparseCore 0:
  40.7 47.1 all-gather.5
  90.0 123.5 all-gather.7
where the time goes:
time: 295 us
  waiting for transfers between devices  182 us (62%)
  blocking collectives  43.7 us (15%)
  starting transfers between devices  32.8 us (11%)
  between operations  14.8 us (5%)
  local copies, waits for them, and re-layouts  8.96 us (3%)
  matrix products  6.08 us (2%)
  other arithmetic  6.06 us (2%)
    all_gather x2, waiting for transfers between devices, all_blocks(): parts = lax.all_gather(parts, axes[k])  152 us
    all_to_all x3, starting transfers between devices, sent_to_all(): return lax.all_to_all(copies, axis, split_axis=0, concat_axis=0, tiled=True)  21.3 us
    all_to_all x1, blocking collectives, on_device(): lax.all_to_all(texts, 'mp', split_axis=0, concat_axis=1, tiled=True)  19.1 us
    all_to_all x3, waiting for transfers between devices, sent_to_all(): return lax.all_to_all(copies, axis, split_axis=0, concat_axis=0, tiled=True)  19.1 us
    all_gather x1, blocking collectives, all_blocks(): parts = lax.all_gather(parts, axes[k])  13.7 us
    all_to_all x1, starting transfers between devices, side_by_side(): lax.all_to_all(both, axis, split_axis=split_dim, concat_axis=concat_dim,...  11.4 us
    all_to_all x1, waiting for transfers between devices, side_by_side(): lax.all_to_all(both, axis, split_axis=split_dim, concat_axis=concat_dim,...  11.1 us
    all_gather x1, blocking collectives, turned_gather(): out = lax.all_gather(both, axis, axis=0, tiled=True)  10.9 us
  transfers between devices with their start and end apart: 6, of which 6 were waited for; matrix products, arithmetic and copies ran while one was open for 2% of the time, Pallas kernels for 0%

commit v1 on v0

v1 whole, which is shorter than its diff:
```python
import functools
import heapq

import jax
import jax.numpy as jnp
from jax import lax
from jax.experimental import pallas as pl
from jax.experimental.pallas import tpu as pltpu
from jax.sharding import Mesh
from jax.sharding import PartitionSpec as P

AXES = ("zl", "x", "y", "zh", "c")
SIZES = (4, 4, 8, 2, 2)
RING = 8
CHUNKS = 3
LOG2E = 1.4426950408889634
LN2 = 0.6931471805599453
TAU, LAT = 0.7, 1.9


def steps_of(chunk, col):
    return (4, 3) if (chunk + col) % 2 else (3, 4)


def schedule(start, busy_up):
    free = {"up": start + busy_up, "down": start, "across": start}
    heap, out, n = [], [], 0

    def send(link, t, item):
        nonlocal n
        begin = max(t, free[link])
        free[link] = begin + TAU
        n += 1
        heapq.heappush(heap, (begin + TAU + LAT, n, item))
        return (link, item)

    def along(t, item):
        chunk, col, d = item
        up, down = steps_of(chunk, col)
        got = []
        if d <= 0 and -d < up:
            got.append(send("up", t, (chunk, col, d - 1)))
        if d >= 0 and d < down:
            got.append(send("down", t, (chunk, col, d + 1)))
        return got

    first = [send("across", start, (c, 1, 0)) for c in (2, 0, 1)]
    for c in (0, 1, 2):
        first += along(start, (c, 0, 0))
    out.append((start, None, first))
    while heap:
        t, _, item = heapq.heappop(heap)
        chunk, col, d = item
        sends = []
        if chunk == 2:
            sends += along(t, item)
        elif col == 0:
            sends += along(t, item)
            sends.append(send("across", t, (chunk, 1, d)))
        out.append((t, item, sends))
    return out


IMAGE_PLAN = schedule(0.0, 2.0)
TEXT_PLAN = schedule(5.0, 0.0)
ITEMS = [item for _, item, _ in IMAGE_PLAN if item is not None]
INDEX = {item: i for i, item in enumerate(ITEMS)}
OWN = [(c, 0, 0) for c in range(CHUNKS)]
ALL = OWN + ITEMS
ALL_INDEX = {item: i for i, item in enumerate(ALL)}


def body(
    images_ref, texts_ref, scale_ref, row_ref, col_ref,
    img, txt, tq, raw, rowbuf, rs, rr, cs, cr, fin_src, fin,
    load_sem, a2a_send, a2a_recv, i_send, i_recv, t_send, t_recv, d_send, d_recv,
    r_send, r_recv, c_send, c_recv, f_send, f_recv,
):
    zl, x, y, zh, c = (lax.axis_index(a) for a in AXES)
    z = zh * 4 + zl
    m = zh * 2 + c
    odd = lax.rem(x, 2)
    xf = x + 1 - 2 * odd
    xg = lax.rem(x + 3 + 2 * odd, 4)
    other = 1 - c

    def at_z(pos):
        return {"zl": lax.rem(pos, 4), "zh": lax.div(pos, 4)}

    def ring(pos, d):
        return lax.rem(pos + (d + RING), RING)

    own_image = (zl * 2 + odd, m)
    own_text = y * 2 + (1 - odd)
    loads = [
        pltpu.make_async_copy(texts_ref, tq, load_sem.at[0]),
        pltpu.make_async_copy(texts_ref.at[m], raw.at[m], load_sem.at[1]),
        pltpu.make_async_copy(images_ref, img.at[own_image[0], own_image[1]], load_sem.at[2]),
    ]
    for load in loads:
        load.start()

    mp_peers = [(dz, dc) for dz in (0, 1) for dc in (0, 1) if dz or dc]

    def mp_of(dz, dc):
        return {"zh": (1 - zh) if dz else zh, "c": other if dc else c}

    links_image = {"up": at_z(ring(z, 1)), "down": at_z(ring(z, -1)), "across": {"x": xf}}
    links_text = {"up": {"y": ring(y, 1)}, "down": {"y": ring(y, -1)}, "across": {"x": xg}}
    barrier = pltpu.get_barrier_semaphore()
    peers = list(links_image.values()) + list(links_text.values()) + [mp_of(*p) for p in mp_peers]
    for peer in peers:
        pl.semaphore_signal(barrier, inc=1, device_id=peer, device_id_type=pl.DeviceIdType.MESH)
    for load in loads:
        load.wait()
    pl.semaphore_wait(barrier, len(peers))

    started = []

    def push(src, dst, send, recv, peer):
        copy = pltpu.make_async_remote_copy(
            src_ref=src, dst_ref=dst, send_sem=send, recv_sem=recv,
            device_id=peer, device_id_type=pl.DeviceIdType.MESH,
        )
        copy.start()
        started.append(copy)
        return copy

    swaps = []
    for n, (dz, dc) in enumerate(mp_peers):
        peer = mp_of(dz, dc)
        theirs = peer["zh"] * 2 + peer["c"]
        swaps.append(push(tq.at[theirs], raw.at[m], a2a_send.at[n], a2a_recv.at[n], peer))

    def image_slot(item, core):
        chunk, col, d = item
        pos = ring(z, d)
        block = lax.rem(pos, 4) * 2 + ((1 - odd) if col else odd)
        return img.at[block, lax.div(pos, 4) * 2 + core, chunk]

    def text_slot(item):
        chunk, col, d = item
        return txt.at[ring(y, d) * 2 + (odd if col else 1 - odd), chunk]

    def moved(link, item):
        chunk, col, d = item
        if link == "across":
            return (chunk, 1 - col, d)
        return (chunk, col, d + 1 if link == "up" else d - 1)

    def hand_over(item):
        n = ALL_INDEX[item]
        push(image_slot(item, c), image_slot(item, c), d_send.at[n], d_recv.at[n], {"c": other})

    def image_event(item, sends):
        if item is not None:
            slot = image_slot(item, c)
            n = INDEX[item]
            pltpu.make_async_remote_copy(
                src_ref=slot, dst_ref=slot, send_sem=i_send.at[n], recv_sem=i_recv.at[n],
                device_id={"c": other}, device_id_type=pl.DeviceIdType.MESH,
            ).wait_recv()
        for link, sent in sends:
            slot = image_slot(moved(link, sent), c)
            n = INDEX[sent]
            push(slot, slot, i_send.at[n], i_recv.at[n], links_image[link])
        for each in [item] if item is not None else OWN:
            hand_over(each)

    def text_event(item, sends):
        if item is not None:
            slot = text_slot(item)
            n = INDEX[item]
            pltpu.make_async_remote_copy(
                src_ref=slot, dst_ref=slot, send_sem=t_send.at[n], recv_sem=t_recv.at[n],
                device_id={"c": other}, device_id_type=pl.DeviceIdType.MESH,
            ).wait_recv()
        else:
            for swap in swaps:
                swap.wait_recv()
            rows = jnp.concatenate([raw[k] for k in range(4)], axis=1).astype(jnp.float32)
            unit = rows * lax.rsqrt(jnp.sum(rows * rows, axis=1, keepdims=True) + 1e-6)
            txt[own_text] = unit.astype(jnp.bfloat16).reshape(CHUNKS, 16, 1024)
        for link, sent in sends:
            slot = text_slot(moved(link, sent))
            n = INDEX[sent]
            push(slot, slot, t_send.at[n], t_recv.at[n], links_text[link])

    events = [(t, 0, n, item, sends) for n, (t, item, sends) in enumerate(IMAGE_PLAN)]
    events += [(t, 1, n, item, sends) for n, (t, item, sends) in enumerate(TEXT_PLAN)]
    for t, kind, _, item, sends in sorted(events, key=lambda e: e[:3]):
        (text_event if kind else image_event)(item, sends)
    for item in ALL:
        slot = image_slot(item, other)
        n = ALL_INDEX[item]
        pltpu.make_async_remote_copy(
            src_ref=slot, dst_ref=slot, send_sem=d_send.at[n], recv_sem=d_recv.at[n],
            device_id={"c": other}, device_id_type=pl.DeviceIdType.MESH,
        ).wait_recv()

    scale = scale_ref[0]

    def rows_of(block):
        parts = [img[block, q].reshape(192, 256) for q in range(4)]
        return jnp.concatenate(parts, axis=1)

    def visit(block, state):
        top, total = state
        rows = rows_of(block)
        wide = rows.astype(jnp.float32)
        factor = lax.rsqrt(jnp.sum(wide * wide, axis=1, keepdims=True) + 1e-6) * (scale * LOG2E)
        scores = factor * lax.dot_general(
            rows, txt[...].reshape(768, 1024), (((1,), (1,)), ((), ())), preferred_element_type=jnp.float32
        )
        row_top = jnp.max(scores, axis=1, keepdims=True)
        row_total = jnp.sum(jnp.exp2(scores - row_top), axis=1, keepdims=True)
        lane = lax.broadcasted_iota(jnp.int32, (192, 128), 1)
        rowbuf[pl.ds(pl.multiple_of(block * 192, 192), 192), :] = jnp.where(lane == 0, row_top, row_total)
        new = jnp.maximum(top, jnp.max(scores, axis=0, keepdims=True))
        total = total * jnp.exp2(top - new) + jnp.sum(jnp.exp2(scores - new), axis=0, keepdims=True)
        return (new, total)

    start = (jnp.full((1, 768), -1e30, jnp.float32), jnp.zeros((1, 768), jnp.float32))
    col_top, col_total = lax.fori_loop(0, 8, visit, start)

    for tb in range(16):
        shift = (768 - tb * 48) % 768
        for k, part in enumerate((col_top, col_total)):
            turned = pltpu.roll(part, shift, 1) if shift else part
            cs[tb, pl.ds(k, 1), :] = turned[:, :128]
    for dy in range(RING):
        for dx in (0, 1):
            n = dy * 2 + dx
            target = ring(y, dy) * 2 + (odd if dx else 1 - odd)
            if n == 0:
                cr[0] = cs[own_text]
            else:
                push(cs.at[target], cr.at[n], c_send.at[n], c_recv.at[n], {"y": ring(y, dy), "x": xg if dx else x})
    for k in range(12):
        turned = jnp.transpose(rowbuf[k * 128 : (k + 1) * 128, :])
        rs[k // 3, :, pl.ds((k % 3) * 128, 128)] = turned[0:2, :]
    for dz in range(RING):
        for dx in (0, 1):
            for dc in (0, 1):
                n = dz * 4 + dx * 2 + dc
                pos = ring(z, dz)
                if n == 0:
                    rr[0] = rs[zl]
                else:
                    push(
                        rs.at[lax.rem(pos, 4)], rr.at[n], r_send.at[n], r_recv.at[n],
                        {**at_z(pos), "x": xf if dx else x, "c": other if dc else c},
                    )

    mine = jnp.concatenate([img[own_image[0], q].reshape(192, 256) for q in range(4)], axis=1).astype(jnp.float32)
    quarters = mine.reshape(4, 48, 1024)
    picked = quarters[0]
    for k in range(1, 4):
        picked = jnp.where(m == k, quarters[k], picked)
    text = txt[own_text].reshape(48, 1024).astype(jnp.float32)
    factor = lax.rsqrt(jnp.sum(picked * picked, axis=1, keepdims=True) + 1e-6) * scale
    matched = factor * jnp.sum(picked * text, axis=1, keepdims=True)
    square = jnp.concatenate([jnp.broadcast_to(matched, (48, 128)), jnp.zeros((80, 128), jnp.float32)], axis=0)
    matched_lanes = jnp.transpose(square)[0:1, :]

    def waits(buf, send, recv, count):
        for n in range(1, count):
            pltpu.make_async_remote_copy(
                src_ref=buf.at[n], dst_ref=buf.at[n], send_sem=send.at[n], recv_sem=recv.at[n],
                device_id={"c": other}, device_id_type=pl.DeviceIdType.MESH,
            ).wait_recv()

    def merged(buf):
        states = buf[...]
        tops, totals = states[:, 0:1, :], states[:, 1:2, :]
        peak = jnp.max(tops, axis=0)
        return (peak + jnp.log2(jnp.sum(totals * jnp.exp2(tops - peak[None]), axis=0))) * LN2

    waits(cr, c_send, c_recv, 16)
    fin_src[0:1, :] = merged(cr)
    fin_src[1:2, :] = matched_lanes
    fin[m] = fin_src[...]
    lasts = []
    for n, (dz, dc) in enumerate(mp_peers):
        lasts.append(push(fin_src, fin.at[m], f_send.at[n], f_recv.at[n], mp_of(dz, dc)))
    waits(rr, r_send, r_recv, 32)
    row_lse = merged(rr)
    row_lse = jnp.where(odd == 0, row_lse, pltpu.roll(row_lse, 192, 1))[:, :256]
    for last in lasts:
        last.wait_recv()
    lane = lax.broadcasted_iota(jnp.int32, (1, 256), 1)
    whole = []
    for k in range(2):
        joined = jnp.zeros((1, 256), jnp.float32)
        for q in range(4):
            part = jnp.concatenate([fin[q, pl.ds(k, 1), :], jnp.zeros((1, 128), jnp.float32)], axis=1)
            part = pltpu.roll(part, q * 48, 1) if q else part
            joined = jnp.where((lane >= q * 48) & (lane < q * 48 + 48), part, joined)
        whole.append(joined)
    row_ref[...] = row_lse - whole[1]
    col_ref[...] = whole[0] - whole[1]
    for copy in started:
        copy.wait_send()


def on_device(images, texts, logit_scale):
    any_space = pl.BlockSpec(memory_space=pl.ANY)
    vmem = pl.BlockSpec(memory_space=pltpu.VMEM)
    dma = pltpu.SemaphoreType.DMA
    bf16, f32 = jnp.bfloat16, jnp.float32
    n_in, n_all = len(ITEMS), len(ALL)
    row, col = pl.pallas_call(
        body,
        out_shape=(jax.ShapeDtypeStruct((1, 256), f32), jax.ShapeDtypeStruct((1, 256), f32)),
        in_specs=[any_space, any_space, pl.BlockSpec(memory_space=pltpu.SMEM)],
        out_specs=(vmem, vmem),
        scratch_shapes=[
            pltpu.VMEM((8, 4, CHUNKS, 64, 256), bf16),
            pltpu.VMEM((16, CHUNKS, 16, 1024), bf16),
            pltpu.VMEM((4, 48, 256), bf16),
            pltpu.VMEM((4, 48, 256), bf16),
            pltpu.VMEM((1536, 128), f32),
            pltpu.VMEM((4, 2, 384), f32),
            pltpu.VMEM((32, 2, 384), f32),
            pltpu.VMEM((16, 2, 128), f32),
            pltpu.VMEM((16, 2, 128), f32),
            pltpu.VMEM((2, 128), f32),
            pltpu.VMEM((4, 2, 128), f32),
            dma((3,)),
            dma((3,)), dma((3,)),
            dma((n_in,)), dma((n_in,)),
            dma((n_in,)), dma((n_in,)),
            dma((n_all,)), dma((n_all,)),
            dma((32,)), dma((32,)),
            dma((16,)), dma((16,)),
            dma((3,)), dma((3,)),
        ],
        compiler_params=pltpu.CompilerParams(collective_id=0, has_side_effects=True),
        name="contrastive",
    )(images.reshape(CHUNKS, 64, 256), texts.reshape(4, 48, 256), logit_scale)
    return row[0, :192], col[0, :192]


def solution(mesh):
    finer = Mesh(mesh.devices.reshape(SIZES), AXES)
    return jax.shard_map(
        on_device,
        mesh=finer,
        in_specs=(P(("zl", "x", "y"), ("zh", "c")), P(("zl", "x", "y"), ("zh", "c")), P()),
        out_specs=(P(("zl", "x", "y")), P(("zl", "x", "y"))),
        check_vma=False,
    )
```

time: 295 us -> 66.8 us (0.23)
  waiting for transfers between devices: 182 us -> 0 us
  Pallas kernels: 0 us -> 63.4 us
  blocking collectives: 43.7 us -> 0 us
  starting transfers between devices: 32.8 us -> 0 us
  between operations: 14.8 us -> 1.29 us
  local copies, waits for them, and re-layouts: 8.96 us -> 1.86 us
  matrix products: 6.08 us -> 0 us
  other arithmetic: 6.06 us -> 0 us
    all_gather x2 -> x0, waiting for transfers between devices: 152 us -> none  [all_blocks(): parts = lax.all_gather(parts, axes[k])]
    pallas_call x0 -> x1, Pallas kernels: none -> 63.4 us  [on_device(): pl.pallas_call(body, out_shape=(jax.ShapeDtypeStruct((1, 256), f32), jax....]
    all_to_all x4 -> x0, starting transfers between devices: 32.7 us -> none  [the longest x3 21.3 us: sent_to_all(): return lax.all_to_all(copies, axis, split_axis=0, concat_axis=0, tiled=True)]
    all_to_all x4 -> x0, waiting for transfers between devices: 30.2 us -> none  [the longest x3 19.1 us: sent_to_all(): return lax.all_to_all(copies, axis, split_axis=0, concat_axis=0, tiled=True)]
    all_gather x2 -> x0, blocking collectives: 24.6 us -> none  [the longest x1 13.7 us: all_blocks(): parts = lax.all_gather(parts, axes[k])]
    all_to_all x1 -> x0, blocking collectives: 19.1 us -> none  [on_device(): lax.all_to_all(texts, 'mp', split_axis=0, concat_axis=1, tiled=True)]
    all_gather x2 -> x0, local copies, waits for them, and re-layouts: 6.28 us -> none  [the longest x1 6.28 us: all_blocks(): parts = lax.all_gather(parts, axes[k])]
    dot_general x1 -> x0, matrix products: 6.08 us -> none  [tile_states(): lax.dot_general(visitor, image_unit, (((1,), (1,)), ((), ())), preferred_...]
  transfers between devices with their start and end apart: 6 -> 0, of which waited for: 6 -> 0; matrix products, arithmetic and copies ran while one was open for 2% -> 0% of each run, Pallas kernels for 0% -> 0%
where the time goes in v1:
time: 66.8 us; the launch traced here: 66.6 us
  Pallas kernels  63.4 us (95%)
  local copies, waits for them, and re-layouts  1.86 us (3%)
  between operations  1.29 us (2%)
    pallas_call x1, Pallas kernels, on_device(): pl.pallas_call(body, out_shape=(jax.ShapeDtypeStruct((1, 256), f32), jax....  63.4 us
    unnamed x6, local copies, waits for them, and re-layouts  1.86 us

profile of v1, /device:TPU:1, one launch (start us, length us, event | category | flops | bytes accessed | tf_op | source)
XLA Modules:
  0.0 66.6 jit_solution(14354280579569585629)
XLA Ops:
  1.3 63.4 %contrastive.1 = (f32[1,256]{1,0:T(1,128)}, f32[1,256]{1,0:T(1,128)}) custom-call(bf16[3,64,256]{2,1,0:T(8,128)(2,1)} %bitcast.6, bf16[4,48,256]{2,1,0:T(8,128)(2,1)} %bitcast.7, f32[1]{0:T(128)S(6)} %copy.7.scale_ref), custom_call_target="tpu_custom_call" | custom-call | tf_op jit(solution)/shard_map/contrastive/pallas_call | solution.py:312
  64.7 0.0 copy-start.1
  64.7 0.7 copy-done.1
  65.4 0.0 copy-start
  65.4 0.6 copy.8
  66.0 0.1 copy-done
  66.0 0.6 copy.9
Async XLA Ops:
  64.7 0.7 %copy-start.1 = (f32[1,256]{1,0:T(1,128)S(1)}, f32[1,256]{1,0:T(1,128)}, u32[]{:S(2)}) copy-start(f32[1,256]{1,0:T(1,128)} %get-tuple-element.4) | copy-start | bytes 3076
  65.4 0.6 copy-start

commit v2 on v0

v2 whole, which is shorter than its diff:
```python
import heapq

import jax
import jax.numpy as jnp
from jax import lax
from jax.experimental import pallas as pl
from jax.experimental.pallas import tpu as pltpu
from jax.sharding import Mesh
from jax.sharding import PartitionSpec as P

AXES = ("zl", "x", "y", "zh", "c")
SIZES = (4, 4, 8, 2, 2)
RING = 8
LOG2E = 1.4426950408889634
LN2 = 0.6931471805599453

PLACES = [(col, d) for col in (0, 1) for d in range(-3, 5)]
ROOT = PLACES.index((0, 0))
IMAGE_TREES = (
    (2, 0, 3, 3, 11, 4, 14, 0, 9, 10, 2, 3, 4, 11, 13, 14),
    (8, 9, 1, 3, 11, 3, 5, 6, 9, 11, 9, 3, 11, 5, 6, 8),
    (1, 3, 10, 3, 12, 13, 7, 1, 9, 1, 3, 3, 3, 12, 13, 7),
)
TEXT_TREES = (
    (8, 3, 3, 3, 3, 4, 14, 15, 1, 10, 2, 3, 13, 14, 3, 14),
    (8, 3, 3, 3, 3, 3, 5, 5, 9, 3, 11, 3, 4, 5, 13, 8),
    (1, 3, 3, 3, 3, 4, 5, 15, 15, 1, 2, 3, 3, 5, 4, 14),
    (8, 3, 3, 3, 3, 4, 5, 1, 1, 1, 2, 3, 13, 11, 13, 9),
    (2, 2, 3, 3, 12, 3, 5, 0, 9, 1, 2, 3, 11, 5, 6, 13),
    (1, 3, 1, 3, 3, 13, 7, 1, 0, 1, 9, 3, 4, 3, 12, 7),
)
IMAGE_KINDS = [(0.0, 0.7)] * 3
TEXT_KINDS = [(1.5, 0.35)] * 3 + [(5.5, 0.35)] * 3
BASE, MORE, FAR, BESIDE, TILE = 2.35, 0.85, 0.5, 2.0, 0.6


def path_of(parent, child):
    (pc, pd), (cc, cd) = PLACES[parent], PLACES[child]
    up = (cd - pd + RING) % RING
    up = up - RING if up > RING // 2 else up
    return (["across"] if pc != cc else []) + (["up"] * up if up > 0 else ["down"] * -up)


def delay_of(path):
    return BASE + MORE * (len(path) - 1) + FAR * (len(path) - path.count("across"))


def plan(trees, kinds, busy):
    free = {"up": busy, "down": busy, "across": 0.0}
    below, weight = [], []
    for kind, tree in enumerate(trees):
        kids = {p: [q for q in range(16) if q != ROOT and tree[q] == p] for p in range(16)}
        deep = {}

        def measure(p):
            deep[p] = max([0.0] + [delay_of(path_of(p, q)) + kinds[kind][1] + measure(q) for q in kids[p]])
            return deep[p]

        measure(ROOT)
        below.append({p: sorted(qs, key=lambda q: -deep[q]) for p, qs in kids.items()})
        weight.append(deep)
    heap = [(kinds[k][0], -weight[k][ROOT], k, ROOT) for k in range(len(trees))]
    heapq.heapify(heap)
    out = []
    while heap:
        t, _, kind, place = heapq.heappop(heap)
        out.append((t, kind, place, below[kind][place]))
        for child in below[kind][place]:
            path = path_of(place, child)
            begin = max(t, free[path[0]])
            ready = begin
            for link in sorted(set(path)):
                first = max(free[link], begin)
                free[link] = first + kinds[kind][1] * path.count(link)
                ready = max(ready, first + kinds[kind][1])
            heapq.heappush(heap, (ready + delay_of(path), -weight[kind][child], kind, child))
    return out


def timeline():
    images, texts = plan(IMAGE_TREES, IMAGE_KINDS, 2.0), plan(TEXT_TREES, TEXT_KINDS, 0.0)
    steps = [(t, "image", kind, place, kids) for t, kind, place, kids in images]
    steps += [(t, "text", kind, place, kids) for t, kind, place, kids in texts]
    image_at = [max(t for t, kind, _, _ in images if kind == k) + BESIDE for k in range(3)]
    text_at = [max(t for t, kind, _, _ in texts if kind % 3 == k) for k in range(3)]
    work = [(t, 0, "rows", i, 0) for i, t in enumerate(image_at)] + [(t, 1, "columns", k, 0) for k, t in enumerate(text_at)]
    work += [(max(image_at[i], text_at[k]), 2, "tile", i, k) for i in range(3) for k in range(3)]
    work += [(max(image_at), 3, "matched", 0, 0)]
    clock = 0.0
    for t, _, what, i, k in sorted(work):
        clock = max(clock, t)
        steps.append((clock, what, i, k, []))
        clock += TILE if what == "tile" else 0.3
    return sorted(steps, key=lambda s: s[0])


STEPS = timeline()


def body(
    images_ref, texts_ref, scale_ref, row_ref, col_ref,
    img, txt, tq, unit, fac, top, total, rs, rr, cs, cr, fin,
    load_sem, a_send, a_recv, i_send, i_recv, t_send, t_recv, d_send, d_recv,
    r_send, r_recv, c_send, c_recv, f_send, f_recv,
):
    zl, x, y, zh, c = (lax.axis_index(a) for a in AXES)
    z = zh * 4 + zl
    m = zh * 2 + c
    odd = lax.rem(x, 2)
    even = 1 - odd
    xf = x + 1 - 2 * odd
    xg = lax.rem(x + 3 + 2 * odd, 4)
    other = 1 - c
    zs = [lax.rem(z + d, RING) for d in range(RING)]
    ys = [lax.rem(y + d, RING) for d in range(RING)]
    z_of = [{"zl": lax.rem(p, 4), "zh": lax.div(p, 4)} for p in zs]
    own_block = zl * 2 + odd
    own_text = y * 2 + even
    loads = [
        pltpu.make_async_copy(texts_ref, tq, load_sem.at[0]),
        pltpu.make_async_copy(texts_ref.at[m], txt.at[own_text, m], load_sem.at[1]),
        pltpu.make_async_copy(images_ref, img.at[own_block, m], load_sem.at[2]),
    ]
    for load in loads:
        load.start()

    mp_peers = [(0, 1), (1, 0), (1, 1)]

    def mp_of(dz, dc):
        return {"zh": (1 - zh) if dz else zh, "c": other if dc else c}

    def hops(trees):
        seen = set()
        for tree in trees:
            for q in range(16):
                if q != ROOT:
                    (pc, pd), (cc, cd) = PLACES[tree[q]], PLACES[q]
                    step = ((cd - pd) % RING, int(pc != cc))
                    seen |= {step, ((-step[0]) % RING, step[1])}
        return sorted(seen)

    def image_peer(step):
        return {**z_of[step[0]], "x": xf if step[1] else x}

    def text_peer(step):
        return {"y": ys[step[0]], "x": xg if step[1] else x}

    peers = [image_peer(s) for s in hops(IMAGE_TREES)] + [text_peer(s) for s in hops(TEXT_TREES)]
    peers += [mp_of(*p) for p in mp_peers if p != (1, 0) or (4, 0) not in hops(IMAGE_TREES)]
    barrier = pltpu.get_barrier_semaphore()
    for peer in peers:
        pl.semaphore_signal(barrier, inc=1, device_id=peer, device_id_type=pl.DeviceIdType.MESH)
    for load in loads:
        load.wait()
    pl.semaphore_wait(barrier, len(peers))

    started = []

    def push(src, dst, send, recv, n, peer):
        copy = pltpu.make_async_remote_copy(
            src_ref=src, dst_ref=dst, send_sem=send.at[n], recv_sem=recv.at[n],
            device_id=peer, device_id_type=pl.DeviceIdType.MESH,
        )
        copy.start()
        started.append(copy)

    def arrived(buf, send, recv, n):
        pltpu.make_async_remote_copy(
            src_ref=buf, dst_ref=buf, send_sem=send.at[n], recv_sem=recv.at[n],
            device_id={"c": other}, device_id_type=pl.DeviceIdType.MESH,
        ).wait_recv()

    for n in (1, 2, 0):
        peer = mp_of(*mp_peers[n])
        push(tq.at[peer["zh"] * 2 + peer["c"]], txt.at[own_text, m], a_send, a_recv, n, peer)

    def image_slot(kind, place, core):
        col, d = PLACES[place]
        pos = z_of[-d % RING]
        return img.at[pos["zl"] * 2 + (even if col else odd), pos["zh"] * 2 + core, kind]

    def text_slot(kind, place):
        col, d = PLACES[place]
        half = zh if kind < 3 else 1 - zh
        return txt.at[ys[-d % RING] * 2 + (odd if col else even), pl.ds(half * 2, 2), kind % 3]

    def step_to(place, child):
        (pc, pd), (cc, cd) = PLACES[place], PLACES[child]
        return ((cd - pd) % RING, int(pc != cc))

    def image_step(kind, place, kids):
        slot = image_slot(kind, place, c)
        if place != ROOT:
            arrived(slot, i_send, i_recv, kind * 16 + place)
        for kid in kids:
            push(slot, slot, i_send, i_recv, kind * 16 + kid, image_peer(step_to(place, kid)))
        push(slot, slot, d_send, d_recv, kind * 16 + place, {"c": other})

    swapped = set()

    def text_step(kind, place, kids):
        slot = text_slot(kind, place)
        if place != ROOT:
            arrived(slot, t_send, t_recv, kind * 16 + place)
        else:
            for n in {0, 1, 2} - swapped if kind >= 3 else {0} - swapped:
                peer = mp_of(*mp_peers[n])
                arrived(txt.at[own_text, peer["zh"] * 2 + peer["c"]], a_send, a_recv, n)
                swapped.add(n)
        for kid in kids:
            push(slot, slot, t_send, t_recv, kind * 16 + kid, text_peer(step_to(place, kid)))

    scale = scale_ref[0]

    def rows_of(i):
        return jnp.concatenate([img[:, q, i].reshape(512, 256) for q in range(4)], axis=1)

    def rows_step(i):
        for place in range(16):
            arrived(image_slot(i, place, other), d_send, d_recv, i * 16 + place)
        wide = rows_of(i).astype(jnp.float32)
        factor = lax.rsqrt(jnp.sum(wide * wide, axis=1, keepdims=True) + 1e-6) * (scale * LOG2E)
        fac[i] = jnp.broadcast_to(factor, (512, 128))

    def columns_step(k):
        wide = jnp.concatenate([txt[:, q, k].reshape(256, 256) for q in range(4)], axis=1).astype(jnp.float32)
        wide = wide * lax.rsqrt(jnp.sum(wide * wide, axis=1, keepdims=True) + 1e-6)
        unit[k] = wide.astype(jnp.bfloat16)

    columns = {}
    seen_rows = set()

    def tile_step(i, k):
        dots = lax.dot_general(rows_of(i), unit[k], (((1,), (1,)), ((), ())), preferred_element_type=jnp.float32)
        factor = fac[i]
        scores = dots * jnp.concatenate([factor, factor], axis=1)
        row_top = jnp.max(scores, axis=1, keepdims=True)
        col_top = jnp.max(scores, axis=0, keepdims=True)
        if i in seen_rows:
            old = top[i]
            new = jnp.maximum(old, row_top)
            part = jnp.sum(jnp.exp2(scores - jnp.concatenate([new, new], axis=1)), axis=1, keepdims=True)
            total[i] = total[i] * jnp.exp2(old - new) + part
        else:
            new = jnp.broadcast_to(row_top, (512, 128))
            part = jnp.sum(jnp.exp2(scores - row_top), axis=1, keepdims=True)
            total[i] = jnp.broadcast_to(part, (512, 128))
        top[i] = new
        seen_rows.add(i)
        if k in columns:
            col_old, col_sum = columns[k]
            col_new = jnp.maximum(col_old, col_top)
            part = jnp.sum(jnp.exp2(scores - col_new), axis=0, keepdims=True)
            columns[k] = (col_new, col_sum * jnp.exp2(col_old - col_new) + part)
        else:
            columns[k] = (col_top, jnp.sum(jnp.exp2(scores - col_top), axis=0, keepdims=True))

    def matched_step():
        got = []
        for g in range(3):
            at = m * 3 + g
            chunk, row = lax.div(at, 4), pl.multiple_of(lax.rem(at, 4) * 16, 16)
            rows = [img[own_block, q, chunk, pl.ds(row, 16), :] for q in range(4)]
            rows = jnp.concatenate(rows, axis=1).astype(jnp.float32)
            text = jnp.concatenate([txt[own_text, q, g] for q in range(4)], axis=1).astype(jnp.float32)
            norms = [lax.rsqrt(jnp.sum(v * v, axis=1, keepdims=True) + 1e-6) for v in (rows, text)]
            got.append(jnp.sum(rows * text, axis=1, keepdims=True) * norms[0] * norms[1] * scale)
        tall = jnp.broadcast_to(jnp.concatenate(got, axis=0), (48, 128))
        square = jnp.concatenate([tall, jnp.zeros((80, 128), jnp.float32)], axis=0)
        fin[m] = jnp.transpose(square)[0:1, :]
        for n in (1, 2, 0):
            push(fin.at[m], fin.at[m], f_send, f_recv, n, mp_of(*mp_peers[n]))

    for _, what, a, b, kids in STEPS:
        if what == "image":
            image_step(a, b, kids)
        elif what == "text":
            text_step(a, b, kids)
        elif what == "rows":
            rows_step(a)
        elif what == "columns":
            columns_step(a)
        elif what == "tile":
            tile_step(a, b)
        else:
            matched_step()

    lane = lax.broadcasted_iota(jnp.int32, (2, 128), 1)
    states = [jnp.concatenate(columns[k], axis=0) for k in range(3)]
    for tb in range(16):
        turned = []
        for k in range(3):
            shift = (256 - tb * 16 + k * 16) % 256
            turned.append((pltpu.roll(states[k], shift, 1) if shift else states[k])[:, :128])
        cs[tb] = jnp.where(lane < 16, turned[0], jnp.where(lane < 32, turned[1], turned[2]))
    for dy in (4, 3, 5, 2, 6, 1, 7, 0):
        for dx in (1, 0):
            for dz, dc in ((1, 1), (1, 0), (0, 1), (0, 0)):
                n = ((dy * 2 + dx) * 2 + dz) * 2 + dc
                source = cs.at[ys[dy] * 2 + (odd if dx else even)]
                if n == 0:
                    cr[m, 0] = source[...]
                else:
                    peer = {**mp_of(dz, dc), "y": ys[dy], "x": xg if dx else x}
                    push(source, cr.at[m, dy * 2 + dx], c_send, c_recv, n, peer)
    lane = lax.broadcasted_iota(jnp.int32, (128, 128), 1)
    for i in range(3):
        for p in range(4):
            rows = pl.ds(p * 128, 128)
            rs[p, i] = jnp.transpose(jnp.where(lane == 0, top[i, rows, :], total[i, rows, :]))[0:2, :]
    for dz in (4, 3, 5, 2, 6, 1, 7, 0):
        for dx in (1, 0):
            for dc in (1, 0):
                n = dz * 4 + dx * 2 + dc
                if n == 0:
                    rr[0] = rs[zl]
                else:
                    peer = {**z_of[dz], "x": xf if dx else x, "c": other if dc else c}
                    push(rs.at[z_of[dz]["zl"]], rr.at[n], r_send, r_recv, n, peer)

    def merged(states):
        tops, totals = states[..., 0:1, :], states[..., 1:2, :]
        peak = jnp.max(tops, axis=0)
        return (peak + jnp.log2(jnp.sum(totals * jnp.exp2(tops - peak[None]), axis=0))) * LN2

    def placed(parts):
        lane = lax.broadcasted_iota(jnp.int32, (1, 256), 1)
        joined = jnp.zeros((1, 256), jnp.float32)
        for q, part in enumerate(parts):
            part = jnp.concatenate([part, jnp.zeros((1, 128), jnp.float32)], axis=1)
            part = pltpu.roll(part, q * 48, 1) if q else part
            joined = jnp.where((lane >= q * 48) & (lane < q * 48 + 48), part, joined)
        return joined

    for n in range(3):
        peer = mp_of(*mp_peers[n])
        arrived(fin.at[peer["zh"] * 2 + peer["c"]], f_send, f_recv, n)
    matched = placed([fin[q] for q in range(4)])
    for n in range(1, 32):
        arrived(rr.at[n], r_send, r_recv, n)
    lse = merged(rr[...])
    lane = lax.broadcasted_iota(jnp.int32, (1, 128), 1)
    kept = [jnp.where(odd == 0, lse[i], pltpu.roll(lse[i], 64, 1)) for i in range(3)]
    front = jnp.where(lane < 64, kept[0], pltpu.roll(kept[1], 64, 1))
    row_ref[...] = jnp.concatenate([front, kept[2]], axis=1) - matched
    for n in range(1, 64):
        dz, dc = (n // 2) % 2, n % 2
        peer = mp_of(dz, dc)
        arrived(cr.at[peer["zh"] * 2 + peer["c"], n // 4], c_send, c_recv, n)
    col_ref[...] = placed([merged(cr[q]) for q in range(4)]) - matched
    for copy in started:
        copy.wait_send()


def on_device(images, texts, logit_scale):
    any_space = pl.BlockSpec(memory_space=pl.ANY)
    vmem = pl.BlockSpec(memory_space=pltpu.VMEM)
    dma = pltpu.SemaphoreType.DMA
    bf16, f32 = jnp.bfloat16, jnp.float32
    row, col = pl.pallas_call(
        body,
        out_shape=(jax.ShapeDtypeStruct((1, 256), f32), jax.ShapeDtypeStruct((1, 256), f32)),
        in_specs=[any_space, any_space, pl.BlockSpec(memory_space=pltpu.SMEM)],
        out_specs=(vmem, vmem),
        scratch_shapes=[
            pltpu.VMEM((8, 4, 3, 64, 256), bf16),
            pltpu.VMEM((16, 4, 3, 16, 256), bf16),
            pltpu.VMEM((4, 3, 16, 256), bf16),
            pltpu.VMEM((3, 256, 1024), bf16),
            pltpu.VMEM((3, 512, 128), f32),
            pltpu.VMEM((3, 512, 128), f32),
            pltpu.VMEM((3, 512, 128), f32),
            pltpu.VMEM((4, 3, 2, 128), f32),
            pltpu.VMEM((32, 3, 2, 128), f32),
            pltpu.VMEM((16, 2, 128), f32),
            pltpu.VMEM((4, 16, 2, 128), f32),
            pltpu.VMEM((4, 1, 128), f32),
            dma((3,)),
            dma((3,)), dma((3,)),
            dma((48,)), dma((48,)),
            dma((96,)), dma((96,)),
            dma((48,)), dma((48,)),
            dma((32,)), dma((32,)),
            dma((64,)), dma((64,)),
            dma((3,)), dma((3,)),
        ],
        compiler_params=pltpu.CompilerParams(collective_id=0, has_side_effects=True),
        name="contrastive",
    )(images.reshape(3, 64, 256), texts.reshape(4, 3, 16, 256), logit_scale)
    return row[0, :192], col[0, :192]


def solution(mesh):
    finer = Mesh(mesh.devices.reshape(SIZES), AXES)
    return jax.shard_map(
        on_device,
        mesh=finer,
        in_specs=(P(("zl", "x", "y"), ("zh", "c")), P(("zl", "x", "y"), ("zh", "c")), P()),
        out_specs=(P(("zl", "x", "y")), P(("zl", "x", "y"))),
        check_vma=False,
    )
```

time: 295 us -> 58.7 us (0.20)
  waiting for transfers between devices: 182 us -> 0 us
  Pallas kernels: 0 us -> 55.3 us
  blocking collectives: 43.7 us -> 0 us
  starting transfers between devices: 32.8 us -> 0 us
  between operations: 14.8 us -> 1.29 us
  local copies, waits for them, and re-layouts: 8.96 us -> 1.86 us
  matrix products: 6.08 us -> 0 us
  other arithmetic: 6.06 us -> 0 us
    all_gather x2 -> x0, waiting for transfers between devices: 152 us -> none  [all_blocks(): parts = lax.all_gather(parts, axes[k])]
    pallas_call x0 -> x1, Pallas kernels: none -> 55.3 us  [on_device(): pl.pallas_call(body, out_shape=(jax.ShapeDtypeStruct((1, 256), f32), jax....]
    all_to_all x4 -> x0, starting transfers between devices: 32.7 us -> none  [the longest x3 21.3 us: sent_to_all(): return lax.all_to_all(copies, axis, split_axis=0, concat_axis=0, tiled=True)]
    all_to_all x4 -> x0, waiting for transfers between devices: 30.2 us -> none  [the longest x3 19.1 us: sent_to_all(): return lax.all_to_all(copies, axis, split_axis=0, concat_axis=0, tiled=True)]
    all_gather x2 -> x0, blocking collectives: 24.6 us -> none  [the longest x1 13.7 us: all_blocks(): parts = lax.all_gather(parts, axes[k])]
    all_to_all x1 -> x0, blocking collectives: 19.1 us -> none  [on_device(): lax.all_to_all(texts, 'mp', split_axis=0, concat_axis=1, tiled=True)]
    all_gather x2 -> x0, local copies, waits for them, and re-layouts: 6.28 us -> none  [the longest x1 6.28 us: all_blocks(): parts = lax.all_gather(parts, axes[k])]
    dot_general x1 -> x0, matrix products: 6.08 us -> none  [tile_states(): lax.dot_general(visitor, image_unit, (((1,), (1,)), ((), ())), preferred_...]
  transfers between devices with their start and end apart: 6 -> 0, of which waited for: 6 -> 0; matrix products, arithmetic and copies ran while one was open for 2% -> 0% of each run, Pallas kernels for 0% -> 0%
where the time goes in v2:
time: 58.7 us; the launch traced here: 58.5 us
  Pallas kernels  55.3 us (94%)
  local copies, waits for them, and re-layouts  1.86 us (3%)
  between operations  1.29 us (2%)
    pallas_call x1, Pallas kernels, on_device(): pl.pallas_call(body, out_shape=(jax.ShapeDtypeStruct((1, 256), f32), jax....  55.3 us
    unnamed x6, local copies, waits for them, and re-layouts  1.86 us

profile of v2, /device:TPU:1, one launch (start us, length us, event | category | flops | bytes accessed | tf_op | source)
XLA Modules:
  0.0 58.5 jit_solution(3435304994855208723)
XLA Ops:
  1.3 55.3 %contrastive.1 = (f32[1,256]{1,0:T(1,128)}, f32[1,256]{1,0:T(1,128)}) custom-call(bf16[3,64,256]{2,1,0:T(8,128)(2,1)} %bitcast.6, bf16[4,3,16,256]{3,2,1,0:T(8,128)(2,1)} %bitcast.7, f32[1]{0:T(128)S(6)} %copy.7.scale_ref), custom_call_target="tpu_custom_call" | custom-call | tf_op jit(solution)/shard_map/contrastive/pallas_call | solution.py:360
  56.6 0.0 copy-start.1
  56.6 0.7 %copy-done.1 = f32[1,256]{1,0:T(1,128)S(1)} copy-done((f32[1,256]{1,0:T(1,128)S(1)}, f32[1,256]{1,0:T(1,128)}, u32[]{:S(2)}) %copy-start.1) | copy-done | bytes 1048
  57.3 0.0 copy-start
  57.3 0.6 copy.8
  57.9 0.1 copy-done
  57.9 0.6 copy.9
Async XLA Ops:
  56.6 0.7 %copy-start.1 = (f32[1,256]{1,0:T(1,128)S(1)}, f32[1,256]{1,0:T(1,128)}, u32[]{:S(2)}) copy-start(f32[1,256]{1,0:T(1,128)} %get-tuple-element.4) | copy-start | bytes 3076
  57.3 0.6 %copy-start = (f32[1,256]{1,0:T(1,128)S(1)}, f32[1,256]{1,0:T(1,128)}, u32[]{:S(2)}) copy-start(f32[1,256]{1,0:T(1,128)} %get-tuple-element.5) | copy-start | bytes 3076

commit v3 on v2

--- a/solution.py
+++ b/solution.py
@@ -17,21 +17,21 @@
 PLACES = [(col, d) for col in (0, 1) for d in range(-3, 5)]
 ROOT = PLACES.index((0, 0))
 IMAGE_TREES = (
-    (2, 0, 3, 3, 11, 4, 14, 0, 9, 10, 2, 3, 4, 11, 13, 14),
-    (8, 9, 1, 3, 11, 3, 5, 6, 9, 11, 9, 3, 11, 5, 6, 8),
-    (1, 3, 10, 3, 12, 13, 7, 1, 9, 1, 3, 3, 3, 12, 13, 7),
+    (1, 2, 3, 3, 5, 6, 3, 15, 15, 1, 2, 3, 11, 5, 6, 6),
+    (9, 2, 3, 3, 11, 4, 5, 1, 9, 1, 2, 3, 11, 12, 13, 7),
+    (3, 0, 10, 3, 11, 4, 0, 6, 0, 10, 11, 3, 11, 12, 6, 8),
 )
 TEXT_TREES = (
-    (8, 3, 3, 3, 3, 4, 14, 15, 1, 10, 2, 3, 13, 14, 3, 14),
-    (8, 3, 3, 3, 3, 3, 5, 5, 9, 3, 11, 3, 4, 5, 13, 8),
-    (1, 3, 3, 3, 3, 4, 5, 15, 15, 1, 2, 3, 3, 5, 4, 14),
-    (8, 3, 3, 3, 3, 4, 5, 1, 1, 1, 2, 3, 13, 11, 13, 9),
-    (2, 2, 3, 3, 12, 3, 5, 0, 9, 1, 2, 3, 11, 5, 6, 13),
-    (1, 3, 1, 3, 3, 13, 7, 1, 0, 1, 9, 3, 4, 3, 12, 7),
+    (3, 3, 3, 3, 3, 3, 5, 6, 15, 1, 11, 3, 3, 3, 6, 0),
+    (3, 2, 10, 3, 5, 12, 7, 0, 0, 10, 3, 3, 11, 3, 13, 7),
+    (1, 3, 10, 3, 3, 3, 5, 0, 0, 1, 3, 3, 4, 5, 8, 7),
+    (2, 0, 3, 3, 11, 3, 5, 6, 15, 10, 11, 3, 4, 5, 6, 5),
+    (1, 3, 10, 3, 3, 4, 3, 6, 0, 0, 11, 3, 4, 12, 6, 14),
+    (1, 3, 1, 3, 12, 13, 7, 1, 9, 1, 2, 3, 3, 12, 12, 9),
 )
 IMAGE_KINDS = [(0.0, 0.7)] * 3
-TEXT_KINDS = [(1.5, 0.35)] * 3 + [(5.5, 0.35)] * 3
-BASE, MORE, FAR, BESIDE, TILE = 2.35, 0.85, 0.5, 2.0, 0.6
+TEXT_KINDS = [(1.5, 0.35)] * 3 + [(6.5, 0.35)] * 3
+BASE, MORE, FAR, BESIDE, TILE, LATE = 3.0, 0.5, 0.0, 2.0, 0.6, 0.8
 
 
 def path_of(parent, child):
@@ -79,8 +79,9 @@
 
 def timeline():
     images, texts = plan(IMAGE_TREES, IMAGE_KINDS, 2.0), plan(TEXT_TREES, TEXT_KINDS, 0.0)
-    steps = [(t, "image", kind, place, kids) for t, kind, place, kids in images]
-    steps += [(t, "text", kind, place, kids) for t, kind, place, kids in texts]
+    steps = [(t, "image", kind, place, kids) for t, kind, place, kids in images if kids]
+    steps += [(t + LATE, "image", kind, place, kids) for t, kind, place, kids in images if not kids]
+    steps += [(t, "text", kind, place, kids) for t, kind, place, kids in texts if kids]
     image_at = [max(t for t, kind, _, _ in images if kind == k) + BESIDE for k in range(3)]
     text_at = [max(t for t, kind, _, _ in texts if kind % 3 == k) for k in range(3)]
     work = [(t, 0, "rows", i, 0) for i, t in enumerate(image_at)] + [(t, 1, "columns", k, 0) for k, t in enumerate(text_at)]
@@ -95,12 +96,22 @@
 
 
 STEPS = timeline()
+TEXT_SEATS = {}
+for kind, tree in enumerate(TEXT_TREES):
+    for place in range(16):
+        if place != ROOT and place in tree:
+            TEXT_SEATS[kind, place] = len(TEXT_SEATS)
+    TEXT_SEATS[kind, None] = len(TEXT_SEATS)
+for kind, tree in enumerate(TEXT_TREES):
+    for place in range(16):
+        if place not in tree:
+            TEXT_SEATS[kind, place] = TEXT_SEATS[kind, None]
 
 
 def body(
-    images_ref, texts_ref, scale_ref, row_ref, col_ref,
+    images_ref, texts_ref, scale_ref, row_ref, col_ref, matched_ref,
     img, txt, tq, unit, fac, top, total, rs, rr, cs, cr, fin,
-    load_sem, a_send, a_recv, i_send, i_recv, t_send, t_recv, d_send, d_recv,
+    load_sem, done_sem, a_send, a_recv, i_send, i_recv, t_send, t_recv, d_send, d_recv,
     r_send, r_recv, c_send, c_recv, f_send, f_recv,
 ):
     zl, x, y, zh, c = (lax.axis_index(a) for a in AXES)
@@ -119,7 +130,7 @@
     loads = [
         pltpu.make_async_copy(texts_ref, tq, load_sem.at[0]),
         pltpu.make_async_copy(texts_ref.at[m], txt.at[own_text, m], load_sem.at[1]),
-        pltpu.make_async_copy(images_ref, img.at[own_block, m], load_sem.at[2]),
+        pltpu.make_async_copy(images_ref, img.at[own_block, zh, c], load_sem.at[2]),
     ]
     for load in loads:
         load.start()
@@ -154,30 +165,32 @@
         load.wait()
     pl.semaphore_wait(barrier, len(peers))
 
-    started = []
-
-    def push(src, dst, send, recv, n, peer):
-        copy = pltpu.make_async_remote_copy(
-            src_ref=src, dst_ref=dst, send_sem=send.at[n], recv_sem=recv.at[n],
+    def push(src, dst, send, recv, peer):
+        pltpu.make_async_remote_copy(
+            src_ref=src, dst_ref=dst, send_sem=send, recv_sem=recv,
             device_id=peer, device_id_type=pl.DeviceIdType.MESH,
-        )
-        copy.start()
-        started.append(copy)
-
-    def arrived(buf, send, recv, n):
+        ).start()
+
+    def arrived(buf, recv):
         pltpu.make_async_remote_copy(
-            src_ref=buf, dst_ref=buf, send_sem=send.at[n], recv_sem=recv.at[n],
+            src_ref=buf, dst_ref=buf, send_sem=done_sem, recv_sem=recv,
             device_id={"c": other}, device_id_type=pl.DeviceIdType.MESH,
         ).wait_recv()
 
+    def sent(buf, send):
+        pltpu.make_async_remote_copy(
+            src_ref=buf, dst_ref=buf, send_sem=send, recv_sem=done_sem,
+            device_id={"c": other}, device_id_type=pl.DeviceIdType.MESH,
+        ).wait_send()
+
     for n in (1, 2, 0):
         peer = mp_of(*mp_peers[n])
-        push(tq.at[peer["zh"] * 2 + peer["c"]], txt.at[own_text, m], a_send, a_recv, n, peer)
+        push(tq.at[peer["zh"] * 2 + peer["c"]], txt.at[own_text, m], a_send, a_recv.at[n], peer)
 
     def image_slot(kind, place, core):
         col, d = PLACES[place]
         pos = z_of[-d % RING]
-        return img.at[pos["zl"] * 2 + (even if col else odd), pos["zh"] * 2 + core, kind]
+        return img.at[pos["zl"] * 2 + (even if col else odd), pos["zh"], core, kind]
 
     def text_slot(kind, place):
         col, d = PLACES[place]
@@ -188,41 +201,47 @@
         (pc, pd), (cc, cd) = PLACES[place], PLACES[child]
         return ((cd - pd) % RING, int(pc != cc))
 
+    def seat(place):
+        return place - (place > ROOT)
+
     def image_step(kind, place, kids):
         slot = image_slot(kind, place, c)
         if place != ROOT:
-            arrived(slot, i_send, i_recv, kind * 16 + place)
+            arrived(slot, i_recv.at[kind * 15 + seat(place)])
         for kid in kids:
-            push(slot, slot, i_send, i_recv, kind * 16 + kid, image_peer(step_to(place, kid)))
-        push(slot, slot, d_send, d_recv, kind * 16 + place, {"c": other})
+            push(slot, slot, i_send.at[kind], i_recv.at[kind * 15 + seat(kid)], image_peer(step_to(place, kid)))
+        push(slot, slot, d_send.at[kind], d_recv.at[kind], {"c": other})
+
 
     swapped = set()
 
     def text_step(kind, place, kids):
         slot = text_slot(kind, place)
         if place != ROOT:
-            arrived(slot, t_send, t_recv, kind * 16 + place)
+            arrived(slot, t_recv.at[TEXT_SEATS[kind, place]])
         else:
             for n in {0, 1, 2} - swapped if kind >= 3 else {0} - swapped:
                 peer = mp_of(*mp_peers[n])
-                arrived(txt.at[own_text, peer["zh"] * 2 + peer["c"]], a_send, a_recv, n)
+                arrived(txt.at[own_text, peer["zh"] * 2 + peer["c"]], a_recv.at[n])
                 swapped.add(n)
         for kid in kids:
-            push(slot, slot, t_send, t_recv, kind * 16 + kid, text_peer(step_to(place, kid)))
+            push(slot, slot, t_send.at[kind], t_recv.at[TEXT_SEATS[kind, kid]], text_peer(step_to(place, kid)))
 
     scale = scale_ref[0]
 
     def rows_of(i):
-        return jnp.concatenate([img[:, q, i].reshape(512, 256) for q in range(4)], axis=1)
+        return jnp.concatenate([img[:, q // 2, q % 2, i].reshape(512, 256) for q in range(4)], axis=1)
 
     def rows_step(i):
-        for place in range(16):
-            arrived(image_slot(i, place, other), d_send, d_recv, i * 16 + place)
+        arrived(img.at[:, :, other, i], d_recv.at[i])
         wide = rows_of(i).astype(jnp.float32)
         factor = lax.rsqrt(jnp.sum(wide * wide, axis=1, keepdims=True) + 1e-6) * (scale * LOG2E)
         fac[i] = jnp.broadcast_to(factor, (512, 128))
 
     def columns_step(k):
+        for kind in (k, k + 3):
+            leaves = sum(q not in TEXT_TREES[kind] for q in range(16))
+            arrived(txt.at[pl.ds(0, leaves), pl.ds(0, 2), k], t_recv.at[TEXT_SEATS[kind, None]])
         wide = jnp.concatenate([txt[:, q, k].reshape(256, 256) for q in range(4)], axis=1).astype(jnp.float32)
         wide = wide * lax.rsqrt(jnp.sum(wide * wide, axis=1, keepdims=True) + 1e-6)
         unit[k] = wide.astype(jnp.bfloat16)
@@ -260,7 +279,7 @@
         for g in range(3):
             at = m * 3 + g
             chunk, row = lax.div(at, 4), pl.multiple_of(lax.rem(at, 4) * 16, 16)
-            rows = [img[own_block, q, chunk, pl.ds(row, 16), :] for q in range(4)]
+            rows = [img[own_block, q // 2, q % 2, chunk, pl.ds(row, 16), :] for q in range(4)]
             rows = jnp.concatenate(rows, axis=1).astype(jnp.float32)
             text = jnp.concatenate([txt[own_text, q, g] for q in range(4)], axis=1).astype(jnp.float32)
             norms = [lax.rsqrt(jnp.sum(v * v, axis=1, keepdims=True) + 1e-6) for v in (rows, text)]
@@ -269,7 +288,7 @@
         square = jnp.concatenate([tall, jnp.zeros((80, 128), jnp.float32)], axis=0)
         fin[m] = jnp.transpose(square)[0:1, :]
         for n in (1, 2, 0):
-            push(fin.at[m], fin.at[m], f_send, f_recv, n, mp_of(*mp_peers[n]))
+            push(fin.at[m], fin.at[m], f_send, f_recv.at[n], mp_of(*mp_peers[n]))
 
     for _, what, a, b, kids in STEPS:
         if what == "image":
@@ -299,10 +318,10 @@
                 n = ((dy * 2 + dx) * 2 + dz) * 2 + dc
                 source = cs.at[ys[dy] * 2 + (odd if dx else even)]
                 if n == 0:
-                    cr[m, 0] = source[...]
+                    cr[m * 16] = source[...]
                 else:
                     peer = {**mp_of(dz, dc), "y": ys[dy], "x": xg if dx else x}
-                    push(source, cr.at[m, dy * 2 + dx], c_send, c_recv, n, peer)
+                    push(source, cr.at[m * 16 + dy * 2 + dx], c_send, c_recv, peer)
     lane = lax.broadcasted_iota(jnp.int32, (128, 128), 1)
     for i in range(3):
         for p in range(4):
@@ -316,7 +335,15 @@
                     rr[0] = rs[zl]
                 else:
                     peer = {**z_of[dz], "x": xf if dx else x, "c": other if dc else c}
-                    push(rs.at[z_of[dz]["zl"]], rr.at[n], r_send, r_recv, n, peer)
+                    push(rs.at[z_of[dz]["zl"]], rr.at[n], r_send, r_recv, peer)
+
+    for k in range(3):
+        sent(img.at[pl.ds(0, 5), 0, 0], i_send.at[k])
+        sent(img.at[:, :, 0, 0], d_send.at[k])
+        for kind in (k, k + 3):
+            sent(txt.at[pl.ds(0, 15), pl.ds(0, 2), 0], t_send.at[kind])
+    sent(tq.at[pl.ds(0, 3)], a_send)
+    sent(fin.at[pl.ds(0, 3)], f_send)
 
     def merged(states):
         tops, totals = states[..., 0:1, :], states[..., 1:2, :]
@@ -334,22 +361,19 @@
 
     for n in range(3):
         peer = mp_of(*mp_peers[n])
-        arrived(fin.at[peer["zh"] * 2 + peer["c"]], f_send, f_recv, n)
+        arrived(fin.at[peer["zh"] * 2 + peer["c"]], f_recv.at[n])
     matched = placed([fin[q] for q in range(4)])
-    for n in range(1, 32):
-        arrived(rr.at[n], r_send, r_recv, n)
+    arrived(rr.at[pl.ds(1, 31)], r_recv)
     lse = merged(rr[...])
     lane = lax.broadcasted_iota(jnp.int32, (1, 128), 1)
     kept = [jnp.where(odd == 0, lse[i], pltpu.roll(lse[i], 64, 1)) for i in range(3)]
     front = jnp.where(lane < 64, kept[0], pltpu.roll(kept[1], 64, 1))
-    row_ref[...] = jnp.concatenate([front, kept[2]], axis=1) - matched
-    for n in range(1, 64):
-        dz, dc = (n // 2) % 2, n % 2
-        peer = mp_of(dz, dc)
-        arrived(cr.at[peer["zh"] * 2 + peer["c"], n // 4], c_send, c_recv, n)
-    col_ref[...] = placed([merged(cr[q]) for q in range(4)]) - matched
-    for copy in started:
-        copy.wait_send()
+    row_ref[...] = jnp.concatenate([front, kept[2]], axis=1)
+    matched_ref[...] = matched
+    arrived(cr.at[pl.ds(1, 63)], c_recv)
+    col_ref[...] = placed([merged(cr[pl.ds(q * 16, 16)]) for q in range(4)])
+    sent(rr.at[pl.ds(1, 31)], r_send)
+    sent(cr.at[pl.ds(1, 63)], c_send)
 
 
 def on_device(images, texts, logit_scale):
@@ -357,13 +381,13 @@
     vmem = pl.BlockSpec(memory_space=pltpu.VMEM)
     dma = pltpu.SemaphoreType.DMA
     bf16, f32 = jnp.bfloat16, jnp.float32
-    row, col = pl.pallas_call(
+    row, col, matched = pl.pallas_call(
         body,
-        out_shape=(jax.ShapeDtypeStruct((1, 256), f32), jax.ShapeDtypeStruct((1, 256), f32)),
+        out_shape=(jax.ShapeDtypeStruct((1, 256), f32),) * 3,
         in_specs=[any_space, any_space, pl.BlockSpec(memory_space=pltpu.SMEM)],
-        out_specs=(vmem, vmem),
+        out_specs=(vmem,) * 3,
         scratch_shapes=[
-            pltpu.VMEM((8, 4, 3, 64, 256), bf16),
+            pltpu.VMEM((8, 2, 2, 3, 64, 256), bf16),
             pltpu.VMEM((16, 4, 3, 16, 256), bf16),
             pltpu.VMEM((4, 3, 16, 256), bf16),
             pltpu.VMEM((3, 256, 1024), bf16),
@@ -373,21 +397,21 @@
             pltpu.VMEM((4, 3, 2, 128), f32),
             pltpu.VMEM((32, 3, 2, 128), f32),
             pltpu.VMEM((16, 2, 128), f32),
-            pltpu.VMEM((4, 16, 2, 128), f32),
+            pltpu.VMEM((64, 2, 128), f32),
             pltpu.VMEM((4, 1, 128), f32),
-            dma((3,)),
+            dma((3,)), dma(()),
+            dma(()), dma((3,)),
+            dma((3,)), dma((45,)),
+            dma((6,)), dma((max(TEXT_SEATS.values()) + 1,)),
             dma((3,)), dma((3,)),
-            dma((48,)), dma((48,)),
-            dma((96,)), dma((96,)),
-            dma((48,)), dma((48,)),
-            dma((32,)), dma((32,)),
-            dma((64,)), dma((64,)),
-            dma((3,)), dma((3,)),
+            dma(()), dma(()),
+            dma(()), dma(()),
+            dma(()), dma((3,)),
         ],
         compiler_params=pltpu.CompilerParams(collective_id=0, has_side_effects=True),
         name="contrastive",
     )(images.reshape(3, 64, 256), texts.reshape(4, 3, 16, 256), logit_scale)
-    return row[0, :192], col[0, :192]
+    return (row - matched)[0, :192], (col - matched)[0, :192]
 
 
 def solution(mesh):

time: 58.7 us -> 52.4 us (0.89)
  Pallas kernels: 55.3 us -> 49.7 us
  local copies, waits for them, and re-layouts: 1.86 us -> 0.67 us
    pallas_call x1, Pallas kernels: 55.3 us -> 49.7 us  [on_device(): pl.pallas_call(body, out_shape=(jax.ShapeDtypeStruct((1, 256), f32),) * 3...]
    unnamed x6, local copies, waits for them, and re-layouts: 1.86 us -> 0.67 us
where the time goes in v3:
time: 52.4 us; the launch traced here: 52.2 us
  Pallas kernels  49.7 us (95%)
  between operations  1.31 us (2%)
  local copies, waits for them, and re-layouts  0.67 us (1%)
  other arithmetic  0.57 us (1%)
    pallas_call x1, Pallas kernels, on_device(): pl.pallas_call(body, out_shape=(jax.ShapeDtypeStruct((1, 256), f32),) * 3...  49.7 us

profile of v3, /device:TPU:1, one launch (start us, length us, event | category | flops | bytes accessed | tf_op | source)
XLA Modules:
  0.0 52.2 jit_solution(10600187990682546112)
XLA Ops:
  1.3 49.7 %contrastive.1 = (f32[1,256]{1,0:T(1,128)}, f32[1,256]{1,0:T(1,128)}, f32[1,256]{1,0:T(1,128)}) custom-call(bf16[3,64,256]{2,1,0:T(8,128)(2,1)} %bitcast.4, bf16[4,3,16,256]{3,2,1,0:T(8,128)(2,1)} %bitcast.5, f32[1]{0:T(128)S(6)} %copy.5.scale_ref), custom_call_target="tpu_custom_call" | custom-call | tf_op jit(solution)/shard_map/contrastive/pallas_call | solution.py:384
  51.0 0.0 copy-start.1
  51.0 0.0 copy-start.2
  51.0 0.0 copy-start
  51.0 0.6 %copy-done.1 = f32[1,256]{1,0:T(1,128)S(1)} copy-done((f32[1,256]{1,0:T(1,128)S(1)}, f32[1,256]{1,0:T(1,128)}, u32[]{:S(2)}) %copy-start.1) | copy-done | bytes 1048
  51.6 0.0 copy-done.2
  51.7 0.0 copy-done
  51.7 0.6 %slice_subtract_fusion = (f32[1,192]{1,0:T(1,128)}, f32[1,192]{1,0:T(1,128)}) fusion(f32[1,256]{1,0:T(1,128)S(1)} %copy-done.1, f32[1,256]{1,0:T(1,128)S(1)} %copy-done.2, f32[1,256]{1,0:T(1,128)S(1)} %copy-done), kind=kLoop, calls=%fused_computation | loop fusion | flops 384 | bytes 3840 | tf_op jit(solution)/shard_map/sub | solution.py:414
Async XLA Ops:
  51.0 0.7 %copy-start.1 = (f32[1,256]{1,0:T(1,128)S(1)}, f32[1,256]{1,0:T(1,128)}, u32[]{:S(2)}) copy-start(f32[1,256]{1,0:T(1,128)} %get-tuple-element.7) | copy-start | bytes 3076
  51.0 0.7 %copy-start.2 = (f32[1,256]{1,0:T(1,128)S(1)}, f32[1,256]{1,0:T(1,128)}, u32[]{:S(2)}) copy-start(f32[1,256]{1,0:T(1,128)} %get-tuple-element.6) | copy-start | bytes 3076
  51.0 0.7 %copy-start = (f32[1,256]{1,0:T(1,128)S(1)}, f32[1,256]{1,0:T(1,128)}, u32[]{:S(2)}) copy-start(f32[1,256]{1,0:T(1,128)} %get-tuple-element.5) | copy-start | bytes 3076

commit v4 on v3

--- a/solution.py
+++ b/solution.py
@@ -31,7 +31,7 @@
 )
 IMAGE_KINDS = [(0.0, 0.7)] * 3
 TEXT_KINDS = [(1.5, 0.35)] * 3 + [(6.5, 0.35)] * 3
-BASE, MORE, FAR, BESIDE, TILE, LATE = 3.0, 0.5, 0.0, 2.0, 0.6, 0.8
+BASE, MORE, FAR, BESIDE, TILE, LATE = 3.0, 0.5, 0.0, 2.0, 0.65, 0.8
 
 
 def path_of(parent, child):
@@ -77,16 +77,27 @@
     return out
 
 
+def by_distance():
+    last = {}
+    for t, _, place, _ in plan(TEXT_TREES, TEXT_KINDS, 0.0):
+        last[place] = max(t, last.get(place, 0.0))
+    order = sorted(last, key=lambda place: last[place])
+    return order[:8], order[8:]
+
+
+NEAR_FAR = by_distance()
+
+
 def timeline():
     images, texts = plan(IMAGE_TREES, IMAGE_KINDS, 2.0), plan(TEXT_TREES, TEXT_KINDS, 0.0)
     steps = [(t, "image", kind, place, kids) for t, kind, place, kids in images if kids]
     steps += [(t + LATE, "image", kind, place, kids) for t, kind, place, kids in images if not kids]
     steps += [(t, "text", kind, place, kids) for t, kind, place, kids in texts if kids]
     image_at = [max(t for t, kind, _, _ in images if kind == k) + BESIDE for k in range(3)]
-    text_at = [max(t for t, kind, _, _ in texts if kind % 3 == k) for k in range(3)]
-    work = [(t, 0, "rows", i, 0) for i, t in enumerate(image_at)] + [(t, 1, "columns", k, 0) for k, t in enumerate(text_at)]
-    work += [(max(image_at[i], text_at[k]), 2, "tile", i, k) for i in range(3) for k in range(3)]
-    work += [(max(image_at), 3, "matched", 0, 0)]
+    text_at = [max(t for t, _, place, _ in texts if place in group) for group in NEAR_FAR]
+    work = [(t, 0, "rows", i, 0) for i, t in enumerate(image_at)]
+    work += [(t, 1, "columns", g, 0) for g, t in enumerate(text_at)]
+    work += [(max(image_at[i], text_at[g]), 2, "tile", i, g) for i in range(3) for g in range(2)]
     clock = 0.0
     for t, _, what, i, k in sorted(work):
         clock = max(clock, t)
@@ -96,21 +107,24 @@
 
 
 STEPS = timeline()
-TEXT_SEATS = {}
+TEXT_SEATS, LEAVES = {}, {}
 for kind, tree in enumerate(TEXT_TREES):
     for place in range(16):
         if place != ROOT and place in tree:
             TEXT_SEATS[kind, place] = len(TEXT_SEATS)
-    TEXT_SEATS[kind, None] = len(TEXT_SEATS)
+N_SEATS = len(TEXT_SEATS)
 for kind, tree in enumerate(TEXT_TREES):
-    for place in range(16):
-        if place not in tree:
-            TEXT_SEATS[kind, place] = TEXT_SEATS[kind, None]
+    for g, group in enumerate(NEAR_FAR):
+        LEAVES[kind, g] = (N_SEATS, sum(place not in tree for place in group))
+        for place in group:
+            if place not in tree:
+                TEXT_SEATS[kind, place] = N_SEATS
+        N_SEATS += 1
 
 
 def body(
     images_ref, texts_ref, scale_ref, row_ref, col_ref, matched_ref,
-    img, txt, tq, unit, fac, top, total, rs, rr, cs, cr, fin,
+    img, txt, tq, unit, fac, held, rs, rr, cs, cr, fin,
     load_sem, done_sem, a_send, a_recv, i_send, i_recv, t_send, t_recv, d_send, d_recv,
     r_send, r_recv, c_send, c_recv, f_send, f_recv,
 ):
@@ -238,13 +252,17 @@
         factor = lax.rsqrt(jnp.sum(wide * wide, axis=1, keepdims=True) + 1e-6) * (scale * LOG2E)
         fac[i] = jnp.broadcast_to(factor, (512, 128))
 
-    def columns_step(k):
-        for kind in (k, k + 3):
-            leaves = sum(q not in TEXT_TREES[kind] for q in range(16))
-            arrived(txt.at[pl.ds(0, leaves), pl.ds(0, 2), k], t_recv.at[TEXT_SEATS[kind, None]])
-        wide = jnp.concatenate([txt[:, q, k].reshape(256, 256) for q in range(4)], axis=1).astype(jnp.float32)
-        wide = wide * lax.rsqrt(jnp.sum(wide * wide, axis=1, keepdims=True) + 1e-6)
-        unit[k] = wide.astype(jnp.bfloat16)
+    def columns_step(g):
+        for kind in range(6):
+            seat, leaves = LEAVES[kind, g]
+            if leaves:
+                arrived(txt.at[pl.ds(0, leaves), pl.ds(0, 2), kind % 3], t_recv.at[seat])
+        for j, place in enumerate(NEAR_FAR[g]):
+            col, d = PLACES[place]
+            at = ys[-d % RING] * 2 + (odd if col else even)
+            wide = jnp.concatenate([txt[at, q].reshape(48, 256) for q in range(4)], axis=1).astype(jnp.float32)
+            wide = wide * lax.rsqrt(jnp.sum(wide * wide, axis=1, keepdims=True) + 1e-6)
+            unit[g, pl.ds(j * 48, 48), :] = wide.astype(jnp.bfloat16)
 
     columns = {}
     seen_rows = set()
@@ -252,19 +270,13 @@
     def tile_step(i, k):
         dots = lax.dot_general(rows_of(i), unit[k], (((1,), (1,)), ((), ())), preferred_element_type=jnp.float32)
         factor = fac[i]
-        scores = dots * jnp.concatenate([factor, factor], axis=1)
+        scores = dots * jnp.concatenate([factor] * 3, axis=1)
         row_top = jnp.max(scores, axis=1, keepdims=True)
         col_top = jnp.max(scores, axis=0, keepdims=True)
-        if i in seen_rows:
-            old = top[i]
-            new = jnp.maximum(old, row_top)
-            part = jnp.sum(jnp.exp2(scores - jnp.concatenate([new, new], axis=1)), axis=1, keepdims=True)
-            total[i] = total[i] * jnp.exp2(old - new) + part
-        else:
-            new = jnp.broadcast_to(row_top, (512, 128))
-            part = jnp.sum(jnp.exp2(scores - row_top), axis=1, keepdims=True)
-            total[i] = jnp.broadcast_to(part, (512, 128))
-        top[i] = new
+        row_total = jnp.sum(jnp.exp2(scores - row_top), axis=1, keepdims=True)
+        lane = lax.broadcasted_iota(jnp.int32, (512, 128), 1)
+        rest = jnp.where(lane == 2 * k + 1, row_total, held[i]) if i in seen_rows else row_total
+        held[i] = jnp.where(lane == 2 * k, row_top, rest)
         seen_rows.add(i)
         if k in columns:
             col_old, col_sum = columns[k]
@@ -299,34 +311,31 @@
             rows_step(a)
         elif what == "columns":
             columns_step(a)
-        elif what == "tile":
+        else:
             tile_step(a, b)
-        else:
-            matched_step()
-
-    lane = lax.broadcasted_iota(jnp.int32, (2, 128), 1)
-    states = [jnp.concatenate(columns[k], axis=0) for k in range(3)]
-    for tb in range(16):
-        turned = []
-        for k in range(3):
-            shift = (256 - tb * 16 + k * 16) % 256
-            turned.append((pltpu.roll(states[k], shift, 1) if shift else states[k])[:, :128])
-        cs[tb] = jnp.where(lane < 16, turned[0], jnp.where(lane < 32, turned[1], turned[2]))
+
+    for g, group in enumerate(NEAR_FAR):
+        states = jnp.concatenate(columns[g], axis=0)
+        for j, place in enumerate(group):
+            cs[place] = (pltpu.roll(states, 384 - j * 48, 1) if j else states)[:, :128]
     for dy in (4, 3, 5, 2, 6, 1, 7, 0):
         for dx in (1, 0):
             for dz, dc in ((1, 1), (1, 0), (0, 1), (0, 0)):
                 n = ((dy * 2 + dx) * 2 + dz) * 2 + dc
-                source = cs.at[ys[dy] * 2 + (odd if dx else even)]
+                source = cs.at[PLACES.index((dx, 4 if dy == 4 else (-dy + 3) % RING - 3))]
                 if n == 0:
                     cr[m * 16] = source[...]
                 else:
                     peer = {**mp_of(dz, dc), "y": ys[dy], "x": xg if dx else x}
                     push(source, cr.at[m * 16 + dy * 2 + dx], c_send, c_recv, peer)
-    lane = lax.broadcasted_iota(jnp.int32, (128, 128), 1)
     for i in range(3):
         for p in range(4):
-            rows = pl.ds(p * 128, 128)
-            rs[p, i] = jnp.transpose(jnp.where(lane == 0, top[i, rows, :], total[i, rows, :]))[0:2, :]
+            turned = jnp.transpose(held[i, pl.ds(p * 128, 128), :])
+            tops = [turned[2 * k : 2 * k + 1, :] for k in range(2)]
+            peak = jnp.maximum(tops[0], tops[1])
+            sums = [turned[2 * k + 1 : 2 * k + 2, :] * jnp.exp2(tops[k] - peak) for k in range(2)]
+            rs[p, i, 0:1, :] = peak
+            rs[p, i, 1:2, :] = sums[0] + sums[1]
     for dz in (4, 3, 5, 2, 6, 1, 7, 0):
         for dx in (1, 0):
             for dc in (1, 0):
@@ -337,13 +346,13 @@
                     peer = {**z_of[dz], "x": xf if dx else x, "c": other if dc else c}
                     push(rs.at[z_of[dz]["zl"]], rr.at[n], r_send, r_recv, peer)
 
+    matched_step()
     for k in range(3):
         sent(img.at[pl.ds(0, 5), 0, 0], i_send.at[k])
         sent(img.at[:, :, 0, 0], d_send.at[k])
         for kind in (k, k + 3):
             sent(txt.at[pl.ds(0, 15), pl.ds(0, 2), 0], t_send.at[kind])
     sent(tq.at[pl.ds(0, 3)], a_send)
-    sent(fin.at[pl.ds(0, 3)], f_send)
 
     def merged(states):
         tops, totals = states[..., 0:1, :], states[..., 1:2, :]
@@ -359,21 +368,22 @@
             joined = jnp.where((lane >= q * 48) & (lane < q * 48 + 48), part, joined)
         return joined
 
-    for n in range(3):
-        peer = mp_of(*mp_peers[n])
-        arrived(fin.at[peer["zh"] * 2 + peer["c"]], f_recv.at[n])
-    matched = placed([fin[q] for q in range(4)])
     arrived(rr.at[pl.ds(1, 31)], r_recv)
     lse = merged(rr[...])
     lane = lax.broadcasted_iota(jnp.int32, (1, 128), 1)
     kept = [jnp.where(odd == 0, lse[i], pltpu.roll(lse[i], 64, 1)) for i in range(3)]
     front = jnp.where(lane < 64, kept[0], pltpu.roll(kept[1], 64, 1))
     row_ref[...] = jnp.concatenate([front, kept[2]], axis=1)
+    for n in range(3):
+        peer = mp_of(*mp_peers[n])
+        arrived(fin.at[peer["zh"] * 2 + peer["c"]], f_recv.at[n])
+    matched = placed([fin[q] for q in range(4)])
     matched_ref[...] = matched
     arrived(cr.at[pl.ds(1, 63)], c_recv)
     col_ref[...] = placed([merged(cr[pl.ds(q * 16, 16)]) for q in range(4)])
     sent(rr.at[pl.ds(1, 31)], r_send)
     sent(cr.at[pl.ds(1, 63)], c_send)
+    sent(fin.at[pl.ds(0, 3)], f_send)
 
 
 def on_device(images, texts, logit_scale):
@@ -390,8 +400,7 @@
             pltpu.VMEM((8, 2, 2, 3, 64, 256), bf16),
             pltpu.VMEM((16, 4, 3, 16, 256), bf16),
             pltpu.VMEM((4, 3, 16, 256), bf16),
-            pltpu.VMEM((3, 256, 1024), bf16),
-            pltpu.VMEM((3, 512, 128), f32),
+            pltpu.VMEM((2, 384, 1024), bf16),
             pltpu.VMEM((3, 512, 128), f32),
             pltpu.VMEM((3, 512, 128), f32),
             pltpu.VMEM((4, 3, 2, 128), f32),
@@ -402,7 +411,7 @@
             dma((3,)), dma(()),
             dma(()), dma((3,)),
             dma((3,)), dma((45,)),
-            dma((6,)), dma((max(TEXT_SEATS.values()) + 1,)),
+            dma((6,)), dma((N_SEATS,)),
             dma((3,)), dma((3,)),
             dma(()), dma(()),
             dma(()), dma(()),

time: 52.4 us -> 51.6 us (0.985)
  Pallas kernels: 49.7 us -> 48.9 us
    pallas_call x1, Pallas kernels: 49.7 us -> 48.9 us  [on_device(): pl.pallas_call(body, out_shape=(jax.ShapeDtypeStruct((1, 256), f32),) * 3...]
where the time goes in v4:
time: 51.6 us; the launch traced here: 51.5 us
  Pallas kernels  48.9 us (95%)
  between operations  1.31 us (3%)
  local copies, waits for them, and re-layouts  0.67 us (1%)
  other arithmetic  0.57 us (1%)
    pallas_call x1, Pallas kernels, on_device(): pl.pallas_call(body, out_shape=(jax.ShapeDtypeStruct((1, 256), f32),) * 3...  48.9 us

profile of v4, /device:TPU:1, one launch (start us, length us, event | category | flops | bytes accessed | tf_op | source)
XLA Modules:
  0.0 51.5 jit_solution(8887844021972692352)
XLA Ops:
  1.3 48.9 %contrastive.1 = (f32[1,256]{1,0:T(1,128)}, f32[1,256]{1,0:T(1,128)}, f32[1,256]{1,0:T(1,128)}) custom-call(bf16[3,64,256]{2,1,0:T(8,128)(2,1)} %bitcast.4, bf16[4,3,16,256]{3,2,1,0:T(8,128)(2,1)} %bitcast.5, f32[1]{0:T(128)S(6)} %copy.5.scale_ref), custom_call_target="tpu_custom_call" | custom-call | tf_op jit(solution)/shard_map/contrastive/pallas_call | solution.py:394
  50.2 0.0 copy-start.1
  50.2 0.0 copy-start.2
  50.2 0.0 copy-start
  50.2 0.6 %copy-done.1 = f32[1,256]{1,0:T(1,128)S(1)} copy-done((f32[1,256]{1,0:T(1,128)S(1)}, f32[1,256]{1,0:T(1,128)}, u32[]{:S(2)}) %copy-start.1) | copy-done | bytes 1048
  50.9 0.0 copy-done.2
  50.9 0.0 copy-done
  50.9 0.6 %slice_subtract_fusion = (f32[1,192]{1,0:T(1,128)}, f32[1,192]{1,0:T(1,128)}) fusion(f32[1,256]{1,0:T(1,128)S(1)} %copy-done.1, f32[1,256]{1,0:T(1,128)S(1)} %copy-done.2, f32[1,256]{1,0:T(1,128)S(1)} %copy-done), kind=kLoop, calls=%fused_computation | loop fusion | flops 384 | bytes 3840 | tf_op jit(solution)/shard_map/sub | solution.py:423
Async XLA Ops:
  50.2 0.7 %copy-start.1 = (f32[1,256]{1,0:T(1,128)S(1)}, f32[1,256]{1,0:T(1,128)}, u32[]{:S(2)}) copy-start(f32[1,256]{1,0:T(1,128)} %get-tuple-element.7) | copy-start | bytes 3076
  50.2 0.7 %copy-start.2 = (f32[1,256]{1,0:T(1,128)S(1)}, f32[1,256]{1,0:T(1,128)}, u32[]{:S(2)}) copy-start(f32[1,256]{1,0:T(1,128)} %get-tuple-element.6) | copy-start | bytes 3076
  50.2 0.7 %copy-start = (f32[1,256]{1,0:T(1,128)S(1)}, f32[1,256]{1,0:T(1,128)}, u32[]{:S(2)}) copy-start(f32[1,256]{1,0:T(1,128)} %get-tuple-element.5) | copy-start | bytes 3076
